TPU v7x, 32 devices: a whole 2x2x4 slice. The times are simulated.
32 devices in a mesh: lat: 2 (over core), lon: 4 (over y, x), lev: 4 (over z).
Axes of the slice: x: 2, y: 2, z: 4, core: 2. Of those that a mesh axis runs over, the one named last changes fastest.
Arguments:
- field_values: float32 [16, 512, 64, 128], P('lat', 'lon', 'lev'), may hold values from 0.2 to 1.8
- crowding: float32 [16, 512, 64, 128], P('lat', 'lon', 'lev'), may hold values from 0.5 to 2
Outputs:
- potential: float32 [16, 512, 64, 128], P('lat', 'lon', 'lev')
- field_values_end: float32 [16, 512, 64, 128], P('lat', 'lon', 'lev')
All inputs are finite; a program needn't handle non-finite values.
Results may differ from a plain program's by a relative error of at most 0.00002.
Values sent between devices are 32-bit elements; how exact they have to be, the bound alone decides.
A program may use at most 256 MiB of HBM per device.

v0:
```python
import functools

import jax
import jax.numpy as jnp
from jax import lax
from jax.experimental import pallas as pl
from jax.experimental.pallas import tpu as pltpu
from jax.sharding import PartitionSpec as P

STEPS = 4
BLOCK = 8


def row_order(rows):
    order = []
    for k in range((rows + 1) // 2):
        order.append(k)
        if rows - 1 - k != k:
            order.append(rows - 1 - k)
    return order


def kernel(
    sizes, f_hbm, c_hbm, pot_hbm, end_hbm,
    field, crowd, lat_lo, lat_hi, lon_lo, lon_hi, lev_lo, lev_hi, face_lo, face_hi, below, sums,
    in_sem, out_sem, lat_send, lat_recv, lon_send, lon_recv, lev_send, lev_recv, sum_send, sum_recv,
):
    Y, X, Z, L = crowd.shape
    order = row_order(Y)
    levels_at = lax.axis_index("lev")
    last = sizes["lev"] - 1
    scale = 1.0 / (Z * sizes["lev"])

    def beside(axis, shift):
        n = sizes[axis]
        return {axis: lax.rem(lax.axis_index(axis) + (shift + n), n)}

    def send(src, dst, send_sem, recv_sem, axis, shift):
        return pltpu.make_async_remote_copy(
            src_ref=src, dst_ref=dst, send_sem=send_sem, recv_sem=recv_sem,
            device_id=beside(axis, shift), device_id_type=pl.DeviceIdType.MESH,
        )

    f_in = [pltpu.make_async_copy(f_hbm.at[y], field.at[0, y, pl.ds(0, X)], in_sem.at[0, y]) for y in range(Y)]
    c_in = [pltpu.make_async_copy(c_hbm.at[y], crowd.at[y], in_sem.at[1, y]) for y in range(Y)]
    for y in order:
        f_in[y].start()
    for y in order:
        c_in[y].start()

    barrier = pltpu.get_barrier_semaphore()
    for axis in ("lat", "lon", "lev"):
        for shift in (-1, 1):
            pl.semaphore_signal(barrier, inc=1, device_id=beside(axis, shift), device_id_type=pl.DeviceIdType.MESH)
    pl.semaphore_wait(barrier, 6)

    def lev_copies(t, y):
        return [
            send(face_lo.at[t, y], lev_hi.at[t, y], lev_send.at[0, t, y], lev_recv.at[0, t, y], "lev", -1),
            send(face_hi.at[t, y], lev_lo.at[t, y], lev_send.at[1, t, y], lev_recv.at[1, t, y], "lev", 1),
        ]

    def lon_copies(t, y):
        row = field.at[t % 2, y]
        return [
            send(row.at[0], lon_hi.at[t, y], lon_send.at[0, t, y], lon_recv.at[0, t, y], "lon", -1),
            send(row.at[X - 1], lon_lo.at[t, y], lon_send.at[1, t, y], lon_recv.at[1, t, y], "lon", 1),
        ]

    def lat_low(t):
        return send(field.at[t % 2, 0, pl.ds(0, X)], lat_hi.at[t], lat_send.at[0, t], lat_recv.at[0, t], "lat", -1)

    def lat_high(t):
        return send(field.at[t % 2, Y - 1, pl.ds(0, X)], lat_lo.at[t], lat_send.at[1, t], lat_recv.at[1, t], "lat", 1)

    def send_row(t, y):
        for copy in lev_copies(t, y) + lon_copies(t, y):
            copy.start()
        if y == 0:
            lat_low(t).start()
        if y == Y - 1:
            lat_high(t).start()

    def sum_copy(y):
        return send(sums.at[y], below.at[y], sum_send.at[y], sum_recv.at[y], "lev", 1)

    for y in order:
        f_in[y].wait()

        @pl.loop(0, X // BLOCK)
        def _(at):
            base = pl.multiple_of(at * BLOCK, BLOCK)
            for i in range(BLOCK):
                face_lo[0, y, pl.ds(base + i, 1), :] = field[0, y, base + i, 0:1, :]
                face_hi[0, y, pl.ds(base + i, 1), :] = field[0, y, base + i, Z - 1 : Z, :]

        send_row(0, y)

    place = lax.broadcasted_iota(jnp.int32, (Z, L), 0)

    for t in range(STEPS):
        now, later = t % 2, (t + 1) % 2
        if t >= 1:
            for y in order:
                for copy in lon_copies(t - 1, y):
                    copy.wait_send()
            lat_low(t - 1).wait_send()
            lat_high(t - 1).wait_send()
        for y in order:
            if t == 0:
                c_in[y].wait()
            if y == 0:
                lat_high(t).wait_recv()
            if y == Y - 1:
                lat_low(t).wait_recv()
            for copy in lon_copies(t, y) + lev_copies(t, y):
                copy.wait_recv()
            before = field.at[now, y - 1] if y > 0 else lat_lo.at[t]
            after = field.at[now, y + 1] if y < Y - 1 else lat_hi.at[t]
            field[now, y, X] = lon_hi[t, y]

            def block(at, carry):
                left, middle = carry
                base = pl.multiple_of(at * BLOCK, BLOCK)
                for i in range(BLOCK):
                    x = base + i
                    right = field[now, y, x + 1]
                    lower = jnp.where(place == 0, lev_lo[t, y, pl.ds(x, 1), :], pltpu.roll(middle, 1, 0))
                    upper = jnp.where(place == Z - 1, lev_hi[t, y, pl.ds(x, 1), :], pltpu.roll(middle, Z - 1, 0))
                    around = (left + right) + (before[x] + after[x]) + (lower + upper)
                    new = 0.1 * around + middle * (0.6 - 0.2 * (middle * crowd[y, x]))
                    field[later, y, x] = new
                    if t < STEPS - 1:
                        face_lo[t + 1, y, pl.ds(x, 1), :] = new[0:1]
                        face_hi[t + 1, y, pl.ds(x, 1), :] = new[Z - 1 : Z]
                    else:
                        shift = 1
                        while shift < Z:
                            new = new + jnp.where(place >= shift, pltpu.roll(new, shift, 0), 0.0)
                            shift *= 2
                        crowd[y, x] = new
                        sums[y, pl.ds(x, 1), :] = new[Z - 1 : Z]
                    left, middle = middle, right
                return left, middle

            lax.fori_loop(0, X // BLOCK, block, (lon_lo[t, y], field[now, y, 0]))
            if t < STEPS - 1:
                send_row(t + 1, y)
            else:
                pltpu.make_async_copy(field.at[later, y, pl.ds(0, X)], end_hbm.at[y], out_sem.at[0, y]).start()

                @pl.when(levels_at == 0)
                def _():
                    sum_copy(y).start()

    @pl.when(levels_at == 0)
    def _():
        below[...] = jnp.zeros_like(below)

    for y in order:
        @pl.when(levels_at > 0)
        def _():
            sum_copy(y).wait_recv()

            @pl.when(levels_at < last)
            def _():
                sums[y] = sums[y] + below[y]
                sum_copy(y).start()

        @pl.loop(0, X // BLOCK)
        def _(at):
            base = pl.multiple_of(at * BLOCK, BLOCK)
            for i in range(BLOCK):
                x = base + i
                crowd[y, x] = (crowd[y, x] + below[y, pl.ds(x, 1), :]) * scale

        pltpu.make_async_copy(crowd.at[y], pot_hbm.at[y], out_sem.at[1, y]).start()

    for y in order:
        @pl.when(levels_at < last)
        def _():
            sum_copy(y).wait_send()

        pltpu.make_async_copy(field.at[STEPS % 2, y, pl.ds(0, X)], end_hbm.at[y], out_sem.at[0, y]).wait()
        pltpu.make_async_copy(crowd.at[y], pot_hbm.at[y], out_sem.at[1, y]).wait()
        for t in range(STEPS):
            for copy in lev_copies(t, y):
                copy.wait_send()
        for copy in lon_copies(STEPS - 1, y):
            copy.wait_send()
    lat_low(STEPS - 1).wait_send()
    lat_high(STEPS - 1).wait_send()


def per_device(sizes, field_values, crowding):
    Y, X, Z, L = field_values.shape
    f32 = jnp.float32
    dma = pltpu.SemaphoreType.DMA
    anywhere = pl.BlockSpec(memory_space=pl.ANY)
    shape = jax.ShapeDtypeStruct(field_values.shape, f32)
    return pl.pallas_call(
        functools.partial(kernel, sizes),
        out_shape=(shape, shape),
        in_specs=[anywhere, anywhere],
        out_specs=(anywhere, anywhere),
        scratch_shapes=[
            pltpu.VMEM((2, Y, X + 1, Z, L), f32),
            pltpu.VMEM((Y, X, Z, L), f32),
            pltpu.VMEM((STEPS, X, Z, L), f32),
            pltpu.VMEM((STEPS, X, Z, L), f32),
            pltpu.VMEM((STEPS, Y, Z, L), f32),
            pltpu.VMEM((STEPS, Y, Z, L), f32),
            pltpu.VMEM((STEPS, Y, X, L), f32),
            pltpu.VMEM((STEPS, Y, X, L), f32),
            pltpu.VMEM((STEPS, Y, X, L), f32),
            pltpu.VMEM((STEPS, Y, X, L), f32),
            pltpu.VMEM((Y, X, L), f32),
            pltpu.VMEM((Y, X, L), f32),
            dma((2, Y)),
            dma((2, Y)),
            dma((2, STEPS)),
            dma((2, STEPS)),
            dma((2, STEPS, Y)),
            dma((2, STEPS, Y)),
            dma((2, STEPS, Y)),
            dma((2, STEPS, Y)),
            dma((Y,)),
            dma((Y,)),
        ],
        compiler_params=pltpu.CompilerParams(
            collective_id=0, has_side_effects=True, vmem_limit_bytes=60 * 1024 * 1024
        ),
    )(field_values, crowding)


def solution(mesh):
    return jax.shard_map(
        functools.partial(per_device, dict(mesh.shape)),
        mesh=mesh,
        in_specs=(P("lat", "lon", "lev", None), P("lat", "lon", "lev", None)),
        out_specs=(P("lat", "lon", "lev", None), P("lat", "lon", "lev", None)),
        check_vma=False,
    )
```

profile of v0, /device:TPU:24, one launch (start us, length us, event | category | flops | bytes accessed | tf_op | source)
XLA Modules:
  0.0 127.5 jit_solution(15941542342593254168)
XLA Ops:
  0.6 115.7 %shard_map.41 = (f32[8,128,16,128]{3,2,1,0:T(8,128)}, f32[8,128,16,128]{3,2,1,0:T(8,128)}) custom-call(f32[8,128,16,128]{3,2,1,0:T(8,128)} %f_hbm.1, f32[8,128,16,128]{3,2,1,0:T(8,128)} %c_hbm.1), custom_call_target="tpu_custom_call" | custom-call | tf_op jit(solution)/shard_map/pallas_call | solution.py:201
  116.4 0.0 copy-start
  116.4 7.7 %copy.6 = f32[8,128,16,128]{3,2,1,0:T(8,128)} copy(f32[8,128,16,128]{3,2,1,0:T(8,128)} %get-tuple-element.4) | data formatting | bytes 16777216
  124.1 0.0 copy-done
  124.1 3.4 %copy.7 = f32[8,128,16,128]{3,2,1,0:T(8,128)} copy(f32[8,128,16,128]{3,2,1,0:T(8,128)S(1)} %copy-done) | data formatting | bytes 16777216
Async XLA Ops:
  116.4 7.7 %copy-start = (f32[8,128,16,128]{3,2,1,0:T(8,128)S(1)}, f32[8,128,16,128]{3,2,1,0:T(8,128)}, u32[]{:S(2)}) copy-start(f32[8,128,16,128]{3,2,1,0:T(8,128)} %get-tuple-element.5) | copy-start | bytes 25165828
where the time goes:
time: 128 us; the launch traced here: 127 us
  Pallas kernels  116 us (91%)
  local copies, waits for them, and re-layouts  11.1 us (9%)
    pallas_call x1, Pallas kernels, per_device(): pl.pallas_call(functools.partial(kernel, sizes), out_shape=(shape, shape)...  116 us
    unnamed x4, local copies, waits for them, and re-layouts  11.1 us

commit v1 on v0

v1 whole, which is shorter than its diff:
```python
import functools

import jax
import jax.numpy as jnp
from jax import lax
from jax.experimental import pallas as pl
from jax.experimental.pallas import tpu as pltpu
from jax.sharding import PartitionSpec as P

STEPS = 4
BLOCK = 8
PIECES = 4
LAG = 2


def row_order(rows):
    order = []
    for k in range((rows + 1) // 2):
        order.append(k)
        if rows - 1 - k != k:
            order.append(rows - 1 - k)
    return order


def march(
    sizes, f_hbm, c_hbm, end, scan, below,
    field, crowd, lat_lo, lat_hi, lon_lo, lon_hi, lev_lo, lev_hi, face_lo, face_hi, sums,
    in_sem, face_sem, lat_send, lat_recv, lon_send, lon_recv, lev_send, lev_recv, sum_send, sum_recv,
):
    Y, X, Z, L = crowd.shape
    order = row_order(Y)
    levels_at = lax.axis_index("lev")
    last = sizes["lev"] - 1

    def beside(axis, shift):
        n = sizes[axis]
        return {axis: lax.rem(lax.axis_index(axis) + (shift + n), n)}

    def send(src, dst, send_sem, recv_sem, axis, shift):
        return pltpu.make_async_remote_copy(
            src_ref=src, dst_ref=dst, send_sem=send_sem, recv_sem=recv_sem,
            device_id=beside(axis, shift), device_id_type=pl.DeviceIdType.MESH,
        )

    def face_in(y):
        return [
            pltpu.make_async_copy(f_hbm.at[y, :, 0], face_lo.at[0, y], face_sem.at[0, y]),
            pltpu.make_async_copy(f_hbm.at[y, :, Z - 1], face_hi.at[0, y], face_sem.at[1, y]),
        ]

    f_in = [pltpu.make_async_copy(f_hbm.at[y], field.at[0, y, pl.ds(0, X)], in_sem.at[0, y]) for y in range(Y)]
    c_in = [pltpu.make_async_copy(c_hbm.at[y], crowd.at[y], in_sem.at[1, y]) for y in range(Y)]
    for y in order[:2]:
        for copy in face_in(y):
            copy.start()
    for at, y in enumerate(order):
        f_in[y].start()
        if at + 2 < Y:
            for copy in face_in(order[at + 2]):
                copy.start()
    for y in order:
        c_in[y].start()

    barrier = pltpu.get_barrier_semaphore()
    for axis in ("lev", "lat", "lon"):
        for shift in (-1, 1):
            pl.semaphore_signal(barrier, inc=1, device_id=beside(axis, shift), device_id_type=pl.DeviceIdType.MESH)
    pl.semaphore_wait(barrier, 6)

    def lev_copies(t, y):
        return [
            send(face_lo.at[t, y], lev_hi.at[t, y], lev_send.at[0, t, y], lev_recv.at[0, t, y], "lev", -1),
            send(face_hi.at[t, y], lev_lo.at[t, y], lev_send.at[1, t, y], lev_recv.at[1, t, y], "lev", 1),
        ]

    def lon_copies(t, y):
        row = field.at[t % 2, y]
        return [
            send(row.at[0], lon_hi.at[t, y], lon_send.at[0, t, y], lon_recv.at[0, t, y], "lon", -1),
            send(row.at[X - 1], lon_lo.at[t, y], lon_send.at[1, t, y], lon_recv.at[1, t, y], "lon", 1),
        ]

    def lat_low(t):
        return send(field.at[t % 2, 0, pl.ds(0, X)], lat_hi.at[t], lat_send.at[0, t], lat_recv.at[0, t], "lat", -1)

    def lat_high(t):
        return send(field.at[t % 2, Y - 1, pl.ds(0, X)], lat_lo.at[t], lat_send.at[1, t], lat_recv.at[1, t], "lat", 1)

    def send_level(t, y):
        for copy in lev_copies(t, y):
            copy.start()

    def send_plane(t, y):
        for copy in lon_copies(t, y):
            copy.start()
        if y == 0:
            lat_low(t).start()
        if y == Y - 1:
            lat_high(t).start()

    piece = X // PIECES

    def sum_copies(y):
        return [
            send(
                sums.at[y, pl.ds(p * piece, piece)], below.at[y, pl.ds(p * piece, piece)],
                sum_send.at[y, p], sum_recv.at[y, p], "lev", 1,
            )
            for p in range(PIECES)
        ]

    def pass_sums(y):
        @pl.when((levels_at > 0) & (levels_at < last))
        def _():
            for p, copy in enumerate(sum_copies(y)):
                copy.wait_recv()
                part = pl.ds(p * piece, piece)
                sums[y, part] = sums[y, part] + below[y, part]
                copy.start()

    for y in order:
        for copy in face_in(y):
            copy.wait()
        send_level(0, y)
    for y in order:
        f_in[y].wait()
        send_plane(0, y)

    @pl.when(levels_at == 0)
    def _():
        below[...] = jnp.zeros_like(below)

    place = lax.broadcasted_iota(jnp.int32, (Z, L), 0)

    for t in range(STEPS):
        now, later = t % 2, (t + 1) % 2
        if t >= 1:
            for y in order:
                for copy in lon_copies(t - 1, y):
                    copy.wait_send()
            lat_low(t - 1).wait_send()
            lat_high(t - 1).wait_send()
        for at, y in enumerate(order):
            if t == 0:
                c_in[y].wait()
            if y == 0:
                lat_high(t).wait_recv()
            if y == Y - 1:
                lat_low(t).wait_recv()
            for copy in lon_copies(t, y) + lev_copies(t, y):
                copy.wait_recv()
            before = field.at[now, y - 1] if y > 0 else lat_lo.at[t]
            after = field.at[now, y + 1] if y < Y - 1 else lat_hi.at[t]
            field[now, y, X] = lon_hi[t, y]

            def block(at, carry):
                left, middle = carry
                base = pl.multiple_of(at * BLOCK, BLOCK)
                for i in range(BLOCK):
                    x = base + i
                    right = field[now, y, x + 1]
                    lower = jnp.where(place == 0, lev_lo[t, y, pl.ds(x, 1), :], pltpu.roll(middle, 1, 0))
                    upper = jnp.where(place == Z - 1, lev_hi[t, y, pl.ds(x, 1), :], pltpu.roll(middle, Z - 1, 0))
                    around = (left + right) + (before[x] + after[x]) + (lower + upper)
                    new = 0.1 * around + middle * (0.6 - 0.2 * (middle * crowd[y, x]))
                    if t < STEPS - 1:
                        field[later, y, x] = new
                        face_lo[t + 1, y, pl.ds(x, 1), :] = new[0:1]
                        face_hi[t + 1, y, pl.ds(x, 1), :] = new[Z - 1 : Z]
                    else:
                        end[y, x] = new
                        shift = 1
                        while shift < Z:
                            new = new + jnp.where(place >= shift, pltpu.roll(new, shift, 0), 0.0)
                            shift *= 2
                        scan[y, x] = new
                        sums[y, pl.ds(x, 1), :] = new[Z - 1 : Z]
                    left, middle = middle, right
                return left, middle

            lax.fori_loop(0, X // BLOCK, block, (lon_lo[t, y], field[now, y, 0]))
            if t < STEPS - 1:
                send_level(t + 1, y)
                send_plane(t + 1, y)
            else:
                @pl.when(levels_at == 0)
                def _():
                    for copy in sum_copies(y):
                        copy.start()

                if at >= LAG:
                    pass_sums(order[at - LAG])

    for y in order[Y - LAG :]:
        pass_sums(y)

    @pl.when(levels_at == last)
    def _():
        for y in order:
            for copy in sum_copies(y):
                copy.wait_recv()

    for y in order:
        @pl.when(levels_at < last)
        def _():
            for copy in sum_copies(y):
                copy.wait_send()

        for t in range(STEPS):
            for copy in lev_copies(t, y):
                copy.wait_send()
        for copy in lon_copies(STEPS - 1, y):
            copy.wait_send()
    lat_low(STEPS - 1).wait_send()
    lat_high(STEPS - 1).wait_send()


def finish(scale, end, scan, below, pot_hbm, end_hbm, pot, out_sem):
    Y, X, Z, L = pot.shape
    ends = [pltpu.make_async_copy(end.at[y], end_hbm.at[y], out_sem.at[0, y]) for y in range(Y)]
    pots = [pltpu.make_async_copy(pot.at[y], pot_hbm.at[y], out_sem.at[1, y]) for y in range(Y)]
    for y in range(Y):
        ends[y].start()
    for y in range(Y):
        @pl.loop(0, X // BLOCK)
        def _(at):
            base = pl.multiple_of(at * BLOCK, BLOCK)
            for i in range(BLOCK):
                x = base + i
                pot[y, x] = (scan[y, x] + below[y, pl.ds(x, 1), :]) * scale

        pots[y].start()
    for y in range(Y):
        ends[y].wait()
        pots[y].wait()


def per_device(sizes, field_values, crowding):
    Y, X, Z, L = field_values.shape
    f32 = jnp.float32
    dma = pltpu.SemaphoreType.DMA
    in_hbm = pl.BlockSpec(memory_space=pltpu.HBM)
    in_vmem = pl.BlockSpec(memory_space=pltpu.VMEM)
    shape = jax.ShapeDtypeStruct(field_values.shape, f32)
    end, scan, below = pl.pallas_call(
        functools.partial(march, sizes),
        out_shape=(pltpu.VMEM((Y, X, Z, L), f32), pltpu.VMEM((Y, X, Z, L), f32), pltpu.VMEM((Y, X, L), f32)),
        in_specs=[in_hbm, in_hbm],
        out_specs=(in_vmem, in_vmem, in_vmem),
        scratch_shapes=[
            pltpu.VMEM((2, Y, X + 1, Z, L), f32),
            pltpu.VMEM((Y, X, Z, L), f32),
            pltpu.VMEM((STEPS, X, Z, L), f32),
            pltpu.VMEM((STEPS, X, Z, L), f32),
            pltpu.VMEM((STEPS, Y, Z, L), f32),
            pltpu.VMEM((STEPS, Y, Z, L), f32),
            pltpu.VMEM((STEPS, Y, X, L), f32),
            pltpu.VMEM((STEPS, Y, X, L), f32),
            pltpu.VMEM((STEPS, Y, X, L), f32),
            pltpu.VMEM((STEPS, Y, X, L), f32),
            pltpu.VMEM((Y, X, L), f32),
            dma((2, Y)),
            dma((2, Y)),
            dma((2, STEPS)),
            dma((2, STEPS)),
            dma((2, STEPS, Y)),
            dma((2, STEPS, Y)),
            dma((2, STEPS, Y)),
            dma((2, STEPS, Y)),
            dma((Y, PIECES)),
            dma((Y, PIECES)),
        ],
        compiler_params=pltpu.CompilerParams(
            collective_id=0, has_side_effects=True, vmem_limit_bytes=43 * 1024 * 1024
        ),
    )(field_values, crowding)
    return pl.pallas_call(
        functools.partial(finish, 1.0 / (Z * sizes["lev"])),
        out_shape=(shape, shape),
        in_specs=[in_vmem, in_vmem, in_vmem],
        out_specs=(in_hbm, in_hbm),
        scratch_shapes=[pltpu.VMEM((Y, X, Z, L), f32), dma((2, Y))],
        compiler_params=pltpu.CompilerParams(vmem_limit_bytes=12 * 1024 * 1024),
    )(end, scan, below)


def solution(mesh):
    return jax.shard_map(
        functools.partial(per_device, dict(mesh.shape)),
        mesh=mesh,
        in_specs=(P("lat", "lon", "lev", None), P("lat", "lon", "lev", None)),
        out_specs=(P("lat", "lon", "lev", None), P("lat", "lon", "lev", None)),
        check_vma=False,
    )
```

time: 128 us -> 121 us (0.945)
  local copies, waits for them, and re-layouts: 11.1 us -> 0 us
  Pallas kernels: 116 us -> 120 us
    unnamed x4 -> x0, local copies, waits for them, and re-layouts: 11.1 us -> none
    pallas_call x1 -> x2, Pallas kernels: 116 us -> 120 us  [the longest x1 114 us: per_device(): pl.pallas_call(functools.partial(march, sizes), out_shape=(pltpu.VMEM((Y,...]
where the time goes in v1:
time: 121 us
  Pallas kernels  120 us (99%)
    pallas_call x1, Pallas kernels, per_device(): pl.pallas_call(functools.partial(march, sizes), out_shape=(pltpu.VMEM((Y,...  114 us
    pallas_call x1, Pallas kernels, per_device(): pl.pallas_call(functools.partial(finish, 1.0 / (Z * sizes['lev'])), out_s...  5.96 us

profile of v1, /device:TPU:24, one launch (start us, length us, event | category | flops | bytes accessed | tf_op | source)
XLA Modules:
  0.0 121.0 jit_solution(11049381479783063016)
XLA Ops:
  0.6 114.4 %shard_map.41 = (f32[8,128,16,128]{3,2,1,0:T(8,128)S(1)}, f32[8,128,16,128]{3,2,1,0:T(8,128)S(1)}, f32[8,128,128]{2,1,0:T(8,128)S(1)}) custom-call(f32[8,128,16,128]{3,2,1,0:T(8,128)} %f_hbm.1, f32[8,128,16,128]{3,2,1,0:T(8,128)} %c_hbm.1), custom_call_target="tpu_custom_call" | custom-call | tf_op jit(solution)/shard_map/pallas_call | solution.py:245
  115.1 6.0 %shard_map.42 = (f32[8,128,16,128]{3,2,1,0:T(8,128)}, f32[8,128,16,128]{3,2,1,0:T(8,128)}) custom-call(f32[8,128,16,128]{3,2,1,0:T(8,128)S(1)} %get-tuple-element.5.end, f32[8,128,16,128]{3,2,1,0:T(8,128)S(1)} %get-tuple-element.6.scan, f32[8,128,128]{2,1,0:T(8,128)S(1)} %get-tuple-element.7.below), custom_call_target="tpu_custom_call" | custom-call | tf_op jit(solution)/shard_map/pallas_call | solution.py:277

commit v2 on v1

v2 whole, which is shorter than its diff:
```python
import functools

import jax
import jax.numpy as jnp
from jax import lax
from jax.experimental import pallas as pl
from jax.experimental.pallas import tpu as pltpu
from jax.sharding import PartitionSpec as P

STEPS = 4
BLOCK = 8


def row_order(rows):
    order = []
    for k in range((rows + 1) // 2):
        order.append(k)
        if rows - 1 - k != k:
            order.append(rows - 1 - k)
    return order


def faces_first(level, rows):
    return min(1 if level == 0 else 2 + 2 * level, rows)


def last_plan(level, levels, rows):
    plan, face = [], faces_first(level, rows)
    behind = 4 * (levels - 2 - level)
    for at in range(rows):
        plan.append(("sum", at))
        if at in (2, 4) and face < rows:
            plan.append(("face", face))
            face += 1
        if level > 0 and 0 <= at - behind:
            plan.append(("top", at - behind))
    plan += [("face", at) for at in range(face, rows)]
    if level > 0:
        plan += [("top", at) for at in range(max(rows - behind, 0), rows)]
    return plan


def march(
    sizes, f_hbm, c_hbm, end, scan, base,
    field, crowd, lat, lon, lev, face, below, sums, top,
    in_sem, face_sem, lat_send, lat_recv, lon_send, lon_recv, lev_send, lev_recv, last_recv,
    top_send, top_recv, sum_send, sum_recv,
):
    Y, X, Z, L = crowd.shape
    order = row_order(Y)
    level = lax.axis_index("lev")
    levels = sizes["lev"]
    LAST = STEPS - 1
    upper_part = jnp.where(level > 0, 0.1, 0.0).astype(jnp.float32)

    def beside(axis, shift):
        n = sizes[axis]
        return {axis: lax.rem(lax.axis_index(axis) + (shift + n), n)}

    def send(src, dst, send_sem, recv_sem, axis, shift):
        return pltpu.make_async_remote_copy(
            src_ref=src, dst_ref=dst, send_sem=send_sem, recv_sem=recv_sem,
            device_id=beside(axis, shift), device_id_type=pl.DeviceIdType.MESH,
        )

    def arrived(ref, sem):
        pltpu.make_async_copy(ref, ref, sem).wait()

    def face_in(rows, group):
        return [
            pltpu.make_async_copy(f_hbm.at[rows, :, 0], face.at[0, 0, rows], face_sem.at[group, 0]),
            pltpu.make_async_copy(f_hbm.at[rows, :, Z - 1], face.at[0, 1, rows], face_sem.at[group, 1]),
        ]

    def field_in(rows, group):
        return pltpu.make_async_copy(f_hbm.at[rows], field.at[0, rows, pl.ds(0, X)], in_sem.at[group])

    inner = pl.ds(1, Y - 2)
    first_faces = face_in(pl.ds(0, 1), 0)
    other_faces = face_in(pl.ds(1, Y - 1), 1)
    f_in = [field_in(pl.ds(0, 1), 0), field_in(pl.ds(Y - 1, 1), 1), field_in(inner, 2)]
    c_in = pltpu.make_async_copy(c_hbm, crowd, in_sem.at[3])
    for copy in first_faces + other_faces + f_in:
        copy.start()
    c_in.start()

    barrier = pltpu.get_barrier_semaphore()
    for axis in ("lev", "lon", "lat"):
        for shift in (-1, 1):
            pl.semaphore_signal(barrier, inc=1, device_id=beside(axis, shift), device_id_type=pl.DeviceIdType.MESH)
    pl.semaphore_wait(barrier, 6)

    def down(t, y, sem):
        return send(face.at[t, 0, y], lev.at[t % 2, y, 1], lev_send.at[t], sem, "lev", -1)

    def up(t, y, sem):
        return send(face.at[t, 1, y], lev.at[t % 2, y, 0], lev_send.at[t], sem, "lev", 1)

    def send_level(t, y):
        up(t, y, lev_recv.at[t % 2, y]).start()
        down(t, y, lev_recv.at[t % 2, y]).start()

    def lon_copies(t, y):
        row = field.at[t % 2, y]
        s = t % 2
        return [
            send(row.at[0], lon.at[s, y, 1], lon_send.at[s], lon_recv.at[s, y], "lon", -1),
            send(row.at[X - 1], lon.at[s, y, 0], lon_send.at[s], lon_recv.at[s, y], "lon", 1),
        ]

    def send_plane(t, y):
        s = t % 2
        for copy in lon_copies(t, y):
            copy.start()
        if y == 0:
            send(field.at[s, 0, pl.ds(0, X)], lat.at[s, 1], lat_send.at[s], lat_recv.at[s], "lat", -1).start()
        if y == Y - 1:
            send(field.at[s, Y - 1, pl.ds(0, X)], lat.at[s, 0], lat_send.at[s], lat_recv.at[s], "lat", 1).start()

    def plane_sent(t):
        arrived(lon.at[t % 2], lon_send.at[t % 2])
        arrived(lat.at[t % 2], lat_send.at[t % 2])

    def rows_beside(t, y):
        before = field.at[t % 2, y - 1] if y > 0 else lat.at[t % 2, 0]
        after = field.at[t % 2, y + 1] if y < Y - 1 else lat.at[t % 2, 1]
        return before, after

    for copy in first_faces:
        copy.wait()
    send_level(0, 0)
    for copy in other_faces:
        copy.wait()
    for y in order[1:]:
        send_level(0, y)
    for copy in f_in:
        copy.wait()
    for y in order:
        send_plane(0, y)

    @pl.when(level == 0)
    def _():
        below[...] = jnp.zeros_like(below)

    c_in.wait()
    place = lax.broadcasted_iota(jnp.int32, (Z, L), 0)

    def step_row(t, y):
        now, later = t % 2, (t + 1) % 2
        if y == 0:
            arrived(lat.at[now], lat_recv.at[now])
        arrived(lon.at[now, y], lon_recv.at[now, y])
        arrived(lev.at[now, y], lev_recv.at[now, y])
        before, after = rows_beside(t, y)
        field[now, y, X] = lon[now, y, 1]

        def block(at, carry):
            left, middle = carry
            start = pl.multiple_of(at * BLOCK, BLOCK)
            for i in range(BLOCK):
                x = start + i
                right = field[now, y, x + 1]
                lower = jnp.where(place == 0, lev[now, y, 0, pl.ds(x, 1), :], pltpu.roll(middle, 1, 0))
                upper = jnp.where(place == Z - 1, lev[now, y, 1, pl.ds(x, 1), :], pltpu.roll(middle, Z - 1, 0))
                around = (left + right) + (before[x] + after[x]) + (lower + upper)
                new = 0.1 * around + middle * (0.6 - 0.2 * (middle * crowd[y, x]))
                field[later, y, x] = new
                face[t + 1, 0, y, pl.ds(x, 1), :] = new[0:1]
                face[t + 1, 1, y, pl.ds(x, 1), :] = new[Z - 1 : Z]
                left, middle = middle, right
            return left, middle

        lax.fori_loop(0, X // BLOCK, block, (lon[now, y, 0], field[now, y, 0]))

    def last_row(y):
        now = LAST % 2
        if y == 0:
            arrived(lat.at[now], lat_recv.at[now])
        arrived(lon.at[now, y], lon_recv.at[now, y])
        before, after = rows_beside(LAST, y)
        field[now, y, X] = lon[now, y, 1]

        def block(at, carry):
            left, middle = carry
            start = pl.multiple_of(at * BLOCK, BLOCK)
            for i in range(BLOCK):
                x = start + i
                right = field[now, y, x + 1]
                lower = jnp.where(place == 0, 0.0, pltpu.roll(middle, 1, 0))
                upper = jnp.where(place == Z - 1, 0.0, pltpu.roll(middle, Z - 1, 0))
                around = (left + right) + (before[x] + after[x]) + (lower + upper)
                new = 0.1 * around + middle * (0.6 - 0.2 * (middle * crowd[y, x]))
                end[y, x] = new
                shift = 1
                while shift < Z:
                    new = new + jnp.where(place >= shift, pltpu.roll(new, shift, 0), 0.0)
                    shift *= 2
                scan[y, x] = new
                sums[y, pl.ds(x, 1), :] = new[Z - 1 : Z]
                left, middle = middle, right
            return left, middle

        lax.fori_loop(0, X // BLOCK, block, (lon[now, y, 0], field[now, y, 0]))

    def sum_copy(y):
        return send(sums.at[y], below.at[y], sum_send, sum_recv.at[y], "lev", 1)

    def send_sum(y, wait):
        if wait:
            sum_copy(y).wait_recv()
        from_below = below[y] + upper_part * face[LAST, 0, y]
        sums[y] = (from_below + 0.1 * face[LAST, 1, y]) + sums[y]
        sum_copy(y).start()

    def last_down(y):
        return down(LAST, y, last_recv.at[1, y])

    def last_up(y):
        return up(LAST, y, last_recv.at[0, y])

    def send_top(y):
        send(face.at[LAST, 1, y], top.at[y], lev_send.at[LAST], top_recv.at[y], "lev", -1).start()

    def relay_top(y):
        copy = send(top.at[y], top.at[y], top_send, top_recv.at[y], "lev", -1)
        copy.wait_recv()
        copy.start()

    for t in range(LAST):
        if t >= 1:
            plane_sent(t - 1)
        for at, y in enumerate(order):
            step_row(t, y)
            if t < LAST - 1:
                send_level(t + 1, y)
            send_plane(t + 1, y)
            if t < LAST - 1:
                continue

            @pl.when(level == levels - 1)
            def _():
                send_top(y)

            @pl.when(level > 0)
            def _():
                last_down(y).start()

            for k in range(1, levels - 1):
                if at < faces_first(k, Y):
                    @pl.when(level == k)
                    def _():
                        last_up(y).start()

            if at < faces_first(0, Y):
                @pl.when(level == 0)
                def _():
                    last_down(y).start()
                    last_up(y).start()

            done = set(order[: at + 1])
            earlier = set(order[:at])
            ready = [
                row for row in order
                if {max(row - 1, 0), row, min(row + 1, Y - 1)} <= done
                and not {max(row - 1, 0), row, min(row + 1, Y - 1)} <= earlier
            ]
            for row in ready:
                last_row(row)
                place_of = order.index(row)

                @pl.when(level == 0)
                def _():
                    send_sum(row, False)
                    plan = last_plan(0, levels, Y)
                    here = plan.index(("sum", place_of))
                    for kind, which in plan[here + 1 : here + 2]:
                        if kind == "face" and place_of < Y - 1:
                            last_down(order[which]).start()
                            last_up(order[which]).start()

    @pl.when(level == 0)
    def _():
        plan = last_plan(0, levels, Y)
        left = [order[which] for kind, which in plan[plan.index(("sum", Y - 1)) + 1 :]]
        for at, y in enumerate(left):
            if at == 0:
                last_down(y).start()
            if at + 1 < len(left):
                last_down(left[at + 1]).start()
            last_up(y).start()

    for k in range(1, levels - 1):
        @pl.when(level == k)
        def _():
            for kind, which in last_plan(k, levels, Y):
                y = order[which]
                if kind == "sum":
                    send_sum(y, True)
                elif kind == "face":
                    last_up(y).start()
                else:
                    relay_top(y)

    now = LAST % 2
    for y in order:
        @pl.when(level == levels - 1)
        def _():
            sum_copy(y).wait_recv()
            top[y] = face[LAST, 1, y]

        @pl.when(level == 0)
        def _():
            arrived(top.at[y], top_recv.at[y])
            lev[now, y, 0] = top[y]

        @pl.when(level > 0)
        def _():
            last_up(y).wait_recv()

        last_down(y).wait_recv()
        base[y] = (below[y] + upper_part * face[LAST, 0, y]) + 0.1 * top[y]

        @pl.loop(0, X // BLOCK)
        def _(at):
            start = pl.multiple_of(at * BLOCK, BLOCK)
            for i in range(BLOCK):
                x = start + i
                upper = 0.1 * lev[now, y, 1, pl.ds(x, 1), :]
                end[y, x, 0:1] = end[y, x, 0:1] + 0.1 * lev[now, y, 0, pl.ds(x, 1), :]
                end[y, x, Z - 1 : Z] = end[y, x, Z - 1 : Z] + upper
                scan[y, x, Z - 1 : Z] = scan[y, x, Z - 1 : Z] + upper

    @pl.when(level < levels - 1)
    def _():
        arrived(sums, sum_send)

    @pl.when((level > 0) & (level < levels - 1))
    def _():
        arrived(top, top_send)

    for t in range(STEPS):
        arrived(face.at[t], lev_send.at[t])
    for t in (LAST - 1, LAST):
        plane_sent(t)


def finish(scale, end, scan, base, pot_hbm, end_hbm, pot, out_sem):
    Y, X, Z, L = pot.shape
    ends = [pltpu.make_async_copy(end.at[y], end_hbm.at[y], out_sem.at[0, y]) for y in range(Y)]
    pots = [pltpu.make_async_copy(pot.at[y], pot_hbm.at[y], out_sem.at[1, y]) for y in range(Y)]
    for y in range(Y):
        ends[y].start()
    for y in range(Y):
        @pl.loop(0, X // BLOCK)
        def _(at):
            start = pl.multiple_of(at * BLOCK, BLOCK)
            for i in range(BLOCK):
                x = start + i
                pot[y, x] = (scan[y, x] + base[y, pl.ds(x, 1), :]) * scale

        pots[y].start()
    for y in range(Y):
        ends[y].wait()
        pots[y].wait()


def per_device(sizes, field_values, crowding):
    Y, X, Z, L = field_values.shape
    f32 = jnp.float32
    dma = pltpu.SemaphoreType.DMA
    in_hbm = pl.BlockSpec(memory_space=pltpu.HBM)
    in_vmem = pl.BlockSpec(memory_space=pltpu.VMEM)
    shape = jax.ShapeDtypeStruct(field_values.shape, f32)
    end, scan, base = pl.pallas_call(
        functools.partial(march, sizes),
        out_shape=(pltpu.VMEM((Y, X, Z, L), f32), pltpu.VMEM((Y, X, Z, L), f32), pltpu.VMEM((Y, X, L), f32)),
        in_specs=[in_hbm, in_hbm],
        out_specs=(in_vmem, in_vmem, in_vmem),
        scratch_shapes=[
            pltpu.VMEM((2, Y, X + 1, Z, L), f32),
            pltpu.VMEM((Y, X, Z, L), f32),
            pltpu.VMEM((2, 2, X, Z, L), f32),
            pltpu.VMEM((2, Y, 2, Z, L), f32),
            pltpu.VMEM((2, Y, 2, X, L), f32),
            pltpu.VMEM((STEPS, 2, Y, X, L), f32),
            pltpu.VMEM((Y, X, L), f32),
            pltpu.VMEM((Y, X, L), f32),
            pltpu.VMEM((Y, X, L), f32),
            dma((4,)),
            dma((2, 2)),
            dma((2,)),
            dma((2,)),
            dma((2,)),
            dma((2, Y)),
            dma((STEPS,)),
            dma((2, Y)),
            dma((2, Y)),
            dma,
            dma((Y,)),
            dma,
            dma((Y,)),
        ],
        compiler_params=pltpu.CompilerParams(
            collective_id=0, has_side_effects=True, vmem_limit_bytes=40 * 1024 * 1024
        ),
    )(field_values, crowding)
    return pl.pallas_call(
        functools.partial(finish, 1.0 / (Z * sizes["lev"])),
        out_shape=(shape, shape),
        in_specs=[in_vmem, in_vmem, in_vmem],
        out_specs=(in_hbm, in_hbm),
        scratch_shapes=[pltpu.VMEM((Y, X, Z, L), f32), dma((2, Y))],
        compiler_params=pltpu.CompilerParams(vmem_limit_bytes=12 * 1024 * 1024),
    )(end, scan, base)


def solution(mesh):
    return jax.shard_map(
        functools.partial(per_device, dict(mesh.shape)),
        mesh=mesh,
        in_specs=(P("lat", "lon", "lev", None), P("lat", "lon", "lev", None)),
        out_specs=(P("lat", "lon", "lev", None), P("lat", "lon", "lev", None)),
        check_vma=False,
    )
```

time: 121 us -> 119 us (0.983)
  the two profiles are of different devices: /device:TPU:24 before, /device:TPU:0 now
where the time goes in v2:
time: 119 us
  Pallas kernels  118 us (99%)
    pallas_call x1, Pallas kernels, per_device(): pl.pallas_call(functools.partial(march, sizes), out_shape=(pltpu.VMEM((Y,...  112 us
    pallas_call x1, Pallas kernels, per_device(): pl.pallas_call(functools.partial(finish, 1.0 / (Z * sizes['lev'])), out_s...  5.96 us

profile of v2, /device:TPU:0, one launch (start us, length us, event | category | flops | bytes accessed | tf_op | source)
XLA Modules:
  0.0 118.8 jit_solution(10485771392250390910)
XLA Ops:
  0.6 112.2 %shard_map.41 = (f32[8,128,16,128]{3,2,1,0:T(8,128)S(1)}, f32[8,128,16,128]{3,2,1,0:T(8,128)S(1)}, f32[8,128,128]{2,1,0:T(8,128)S(1)}) custom-call(f32[8,128,16,128]{3,2,1,0:T(8,128)} %f_hbm.1, f32[8,128,16,128]{3,2,1,0:T(8,128)} %c_hbm.1), custom_call_target="tpu_custom_call" | custom-call | tf_op jit(solution)/shard_map/pallas_call | solution.py:374
  112.9 6.0 %shard_map.42 = (f32[8,128,16,128]{3,2,1,0:T(8,128)}, f32[8,128,16,128]{3,2,1,0:T(8,128)}) custom-call(f32[8,128,16,128]{3,2,1,0:T(8,128)S(1)} %get-tuple-element.5.end, f32[8,128,16,128]{3,2,1,0:T(8,128)S(1)} %get-tuple-element.6.scan, f32[8,128,128]{2,1,0:T(8,128)S(1)} %get-tuple-element.7.base), custom_call_target="tpu_custom_call" | custom-call | tf_op jit(solution)/shard_map/pallas_call | solution.py:407

commit v3 on v2

--- a/solution.py
+++ b/solution.py
@@ -24,26 +24,34 @@
     return min(1 if level == 0 else 2 + 2 * level, rows)
 
 
+def tops_before(level, levels, rows, at):
+    if level == levels - 2:
+        return min(at + 3, rows)
+    if level == levels - 3:
+        return max(min(2 * (at - 3), rows - 2), 0)
+    return 0
+
+
 def last_plan(level, levels, rows):
-    plan, face = [], faces_first(level, rows)
-    behind = 4 * (levels - 2 - level)
+    plan, face, top = [], faces_first(level, rows), 0
     for at in range(rows):
+        while level > 0 and top < tops_before(level, levels, rows, at):
+            plan.append(("top", top))
+            top += 1
         plan.append(("sum", at))
         if at in (2, 4) and face < rows:
             plan.append(("face", face))
             face += 1
-        if level > 0 and 0 <= at - behind:
-            plan.append(("top", at - behind))
     plan += [("face", at) for at in range(face, rows)]
     if level > 0:
-        plan += [("top", at) for at in range(max(rows - behind, 0), rows)]
+        plan += [("top", at) for at in range(top, rows)]
     return plan
 
 
 def march(
     sizes, f_hbm, c_hbm, end, scan, base,
     field, crowd, lat, lon, lev, face, below, sums, top,
-    in_sem, face_sem, lat_send, lat_recv, lon_send, lon_recv, lev_send, lev_recv, last_recv,
+    in_sem, face_sem, lat_send, lat_recv, lon_send, lon_recv, lev_send, lev_recv,
     top_send, top_recv, sum_send, sum_recv,
 ):
     Y, X, Z, L = crowd.shape
@@ -213,10 +221,10 @@
         sum_copy(y).start()
 
     def last_down(y):
-        return down(LAST, y, last_recv.at[1, y])
+        return down(LAST, y, lev_recv.at[LAST % 2, y])
 
     def last_up(y):
-        return up(LAST, y, last_recv.at[0, y])
+        return up(LAST, y, lev_recv.at[LAST % 2, y])
 
     def send_top(y):
         send(face.at[LAST, 1, y], top.at[y], lev_send.at[LAST], top_recv.at[y], "lev", -1).start()
@@ -312,23 +320,21 @@
         def _():
             arrived(top.at[y], top_recv.at[y])
             lev[now, y, 0] = top[y]
+            last_down(y).wait_recv()
 
         @pl.when(level > 0)
         def _():
-            last_up(y).wait_recv()
-
-        last_down(y).wait_recv()
+            arrived(lev.at[now, y], lev_recv.at[now, y])
+
         base[y] = (below[y] + upper_part * face[LAST, 0, y]) + 0.1 * top[y]
 
         @pl.loop(0, X // BLOCK)
         def _(at):
-            start = pl.multiple_of(at * BLOCK, BLOCK)
-            for i in range(BLOCK):
-                x = start + i
-                upper = 0.1 * lev[now, y, 1, pl.ds(x, 1), :]
-                end[y, x, 0:1] = end[y, x, 0:1] + 0.1 * lev[now, y, 0, pl.ds(x, 1), :]
-                end[y, x, Z - 1 : Z] = end[y, x, Z - 1 : Z] + upper
-                scan[y, x, Z - 1 : Z] = scan[y, x, Z - 1 : Z] + upper
+            some = pl.ds(pl.multiple_of(at * BLOCK, BLOCK), BLOCK)
+            upper = 0.1 * lev[now, y, 1, some, :]
+            end[y, some, 0, :] = end[y, some, 0, :] + 0.1 * lev[now, y, 0, some, :]
+            end[y, some, Z - 1, :] = end[y, some, Z - 1, :] + upper
+            scan[y, some, Z - 1, :] = scan[y, some, Z - 1, :] + upper
 
     @pl.when(level < levels - 1)
     def _():
@@ -346,10 +352,8 @@
 
 def finish(scale, end, scan, base, pot_hbm, end_hbm, pot, out_sem):
     Y, X, Z, L = pot.shape
-    ends = [pltpu.make_async_copy(end.at[y], end_hbm.at[y], out_sem.at[0, y]) for y in range(Y)]
-    pots = [pltpu.make_async_copy(pot.at[y], pot_hbm.at[y], out_sem.at[1, y]) for y in range(Y)]
-    for y in range(Y):
-        ends[y].start()
+    ends = pltpu.make_async_copy(end, end_hbm, out_sem.at[0])
+    ends.start()
     for y in range(Y):
         @pl.loop(0, X // BLOCK)
         def _(at):
@@ -358,10 +362,9 @@
                 x = start + i
                 pot[y, x] = (scan[y, x] + base[y, pl.ds(x, 1), :]) * scale
 
-        pots[y].start()
-    for y in range(Y):
-        ends[y].wait()
-        pots[y].wait()
+        pltpu.make_async_copy(pot.at[y], pot_hbm.at[y], out_sem.at[1]).start()
+    ends.wait()
+    pltpu.make_async_copy(pot, pot_hbm, out_sem.at[1]).wait()
 
 
 def per_device(sizes, field_values, crowding):
@@ -394,7 +397,6 @@
             dma((2, Y)),
             dma((STEPS,)),
             dma((2, Y)),
-            dma((2, Y)),
             dma,
             dma((Y,)),
             dma,
@@ -409,7 +411,7 @@
         out_shape=(shape, shape),
         in_specs=[in_vmem, in_vmem, in_vmem],
         out_specs=(in_hbm, in_hbm),
-        scratch_shapes=[pltpu.VMEM((Y, X, Z, L), f32), dma((2, Y))],
+        scratch_shapes=[pltpu.VMEM((Y, X, Z, L), f32), dma((2,))],
         compiler_params=pltpu.CompilerParams(vmem_limit_bytes=12 * 1024 * 1024),
     )(end, scan, base)
 

time: 119 us -> 114 us (0.958)
  the two profiles are of different devices: /device:TPU:0 before, /device:TPU:24 now
where the time goes in v3:
time: 114 us; the launch traced here: 113 us
  Pallas kernels  112 us (98%)
    pallas_call x1, Pallas kernels, per_device(): pl.pallas_call(functools.partial(march, sizes), out_shape=(pltpu.VMEM((Y,...  106 us
    pallas_call x1, Pallas kernels, per_device(): pl.pallas_call(functools.partial(finish, 1.0 / (Z * sizes['lev'])), out_s...  5.96 us

profile of v3, /device:TPU:24, one launch (start us, length us, event | category | flops | bytes accessed | tf_op | source)
XLA Modules:
  0.0 112.7 jit_solution(5732438283590309287)
XLA Ops:
  0.6 106.1 %shard_map.41 = (f32[8,128,16,128]{3,2,1,0:T(8,128)S(1)}, f32[8,128,16,128]{3,2,1,0:T(8,128)S(1)}, f32[8,128,128]{2,1,0:T(8,128)S(1)}) custom-call(f32[8,128,16,128]{3,2,1,0:T(8,128)} %f_hbm.1, f32[8,128,16,128]{3,2,1,0:T(8,128)} %c_hbm.1), custom_call_target="tpu_custom_call" | custom-call | tf_op jit(solution)/shard_map/pallas_call | solution.py:377
  106.7 6.0 %shard_map.42 = (f32[8,128,16,128]{3,2,1,0:T(8,128)}, f32[8,128,16,128]{3,2,1,0:T(8,128)}) custom-call(f32[8,128,16,128]{3,2,1,0:T(8,128)S(1)} %get-tuple-element.5.end, f32[8,128,16,128]{3,2,1,0:T(8,128)S(1)} %get-tuple-element.6.scan, f32[8,128,128]{2,1,0:T(8,128)S(1)} %get-tuple-element.7.base), custom_call_target="tpu_custom_call" | custom-call | tf_op jit(solution)/shard_map/pallas_call | solution.py:409

commit v4 on v3

--- a/solution.py
+++ b/solution.py
@@ -9,6 +9,7 @@
 
 STEPS = 4
 BLOCK = 8
+PIECE = 64
 
 
 def row_order(rows):
@@ -52,7 +53,7 @@
     sizes, f_hbm, c_hbm, end, scan, base,
     field, crowd, lat, lon, lev, face, below, sums, top,
     in_sem, face_sem, lat_send, lat_recv, lon_send, lon_recv, lev_send, lev_recv,
-    top_send, top_recv, sum_send, sum_recv,
+    top_send, top_recv, sum_send, sum_recv, ends_sem,
 ):
     Y, X, Z, L = crowd.shape
     order = row_order(Y)
@@ -92,11 +93,53 @@
         copy.start()
     c_in.start()
 
+    places = {axis: lax.axis_index(axis) for axis in ("lev", "lon")}
     barrier = pltpu.get_barrier_semaphore()
-    for axis in ("lev", "lon", "lat"):
-        for shift in (-1, 1):
-            pl.semaphore_signal(barrier, inc=1, device_id=beside(axis, shift), device_id_type=pl.DeviceIdType.MESH)
-    pl.semaphore_wait(barrier, 6)
+
+    def signal(sem, axis, shift):
+        pl.semaphore_signal(sem, inc=1, device_id=beside(axis, shift), device_id_type=pl.DeviceIdType.MESH)
+
+    greeted = 1
+    for axis, place in places.items():
+        @pl.when(place > 0)
+        def _():
+            signal(barrier, axis, -1)
+
+        @pl.when(place < sizes[axis] - 1)
+        def _():
+            signal(barrier, axis, 1)
+
+        greeted += jnp.where(place > 0, 1, 0) + jnp.where(place < sizes[axis] - 1, 1, 0)
+    signal(barrier, "lat", 1)
+    pl.semaphore_wait(barrier, greeted)
+
+    for at, (axis, place) in enumerate(places.items()):
+        @pl.when(place == 0)
+        def _():
+            signal(ends_sem.at[at, 0], axis, 1)
+
+        @pl.when(place == sizes[axis] - 1)
+        def _():
+            signal(ends_sem.at[at, 1], axis, -1)
+
+    def meet_ends(axis):
+        at, place = list(places).index(axis), places[axis]
+
+        @pl.when(place > 0)
+        def _():
+            pl.semaphore_wait(ends_sem.at[at, 0], 1)
+
+            @pl.when(place < sizes[axis] - 1)
+            def _():
+                signal(ends_sem.at[at, 0], axis, 1)
+
+        @pl.when(place < sizes[axis] - 1)
+        def _():
+            pl.semaphore_wait(ends_sem.at[at, 1], 1)
+
+            @pl.when(place > 0)
+            def _():
+                signal(ends_sem.at[at, 1], axis, -1)
 
     def down(t, y, sem):
         return send(face.at[t, 0, y], lev.at[t % 2, y, 1], lev_send.at[t], sem, "lev", -1)
@@ -134,15 +177,42 @@
         after = field.at[t % 2, y + 1] if y < Y - 1 else lat.at[t % 2, 1]
         return before, after
 
+    def start_level(y, wrap):
+        @pl.when((level == levels - 1) if wrap else (level < levels - 1))
+        def _():
+            up(0, y, lev_recv.at[0, y]).start()
+
+        @pl.when((level == 0) if wrap else (level > 0))
+        def _():
+            down(0, y, lev_recv.at[0, y]).start()
+
     for copy in first_faces:
         copy.wait()
-    send_level(0, 0)
+    start_level(0, False)
     for copy in other_faces:
         copy.wait()
-    for y in order[1:]:
-        send_level(0, y)
+    ahead = Y // 2
+    for y in order[1:ahead]:
+        start_level(y, False)
+
+    @pl.when((level > 0) & (level < levels - 1))
+    def _():
+        for y in order[ahead:]:
+            start_level(y, False)
+
+    meet_ends("lev")
+
+    @pl.when((level == 0) | (level == levels - 1))
+    def _():
+        for y in order[:ahead]:
+            start_level(y, True)
+        for y in order[ahead:]:
+            start_level(y, False)
+            start_level(y, True)
+
     for copy in f_in:
         copy.wait()
+    meet_ends("lon")
     for y in order:
         send_plane(0, y)
 
@@ -328,9 +398,8 @@
 
         base[y] = (below[y] + upper_part * face[LAST, 0, y]) + 0.1 * top[y]
 
-        @pl.loop(0, X // BLOCK)
-        def _(at):
-            some = pl.ds(pl.multiple_of(at * BLOCK, BLOCK), BLOCK)
+        for start in range(0, X, PIECE):
+            some = pl.ds(start, PIECE)
             upper = 0.1 * lev[now, y, 1, some, :]
             end[y, some, 0, :] = end[y, some, 0, :] + 0.1 * lev[now, y, 0, some, :]
             end[y, some, Z - 1, :] = end[y, some, Z - 1, :] + upper
@@ -401,6 +470,7 @@
             dma((Y,)),
             dma,
             dma((Y,)),
+            pltpu.SemaphoreType.REGULAR((2, 2)),
         ],
         compiler_params=pltpu.CompilerParams(
             collective_id=0, has_side_effects=True, vmem_limit_bytes=40 * 1024 * 1024

time: 114 us -> 113 us (level); the launches traced: 113 us -> 113 us
  no operation moved by 1% of the time
where the time goes in v4:
time: 113 us
  Pallas kernels  112 us (99%)
    pallas_call x1, Pallas kernels, per_device(): pl.pallas_call(functools.partial(march, sizes), out_shape=(pltpu.VMEM((Y,...  106 us
    pallas_call x1, Pallas kernels, per_device(): pl.pallas_call(functools.partial(finish, 1.0 / (Z * sizes['lev'])), out_s...  5.96 us

profile of v4, /device:TPU:24, one launch (start us, length us, event | category | flops | bytes accessed | tf_op | source)
XLA Modules:
  0.0 113.1 jit_solution(6763006905972783008)
XLA Ops:
  0.6 106.5 %shard_map.41 = (f32[8,128,16,128]{3,2,1,0:T(8,128)S(1)}, f32[8,128,16,128]{3,2,1,0:T(8,128)S(1)}, f32[8,128,128]{2,1,0:T(8,128)S(1)}) custom-call(f32[8,128,16,128]{3,2,1,0:T(8,128)} %f_hbm.1, f32[8,128,16,128]{3,2,1,0:T(8,128)} %c_hbm.1), custom_call_target="tpu_custom_call" | custom-call | tf_op jit(solution)/shard_map/pallas_call | solution.py:446
  107.1 6.0 %shard_map.42 = (f32[8,128,16,128]{3,2,1,0:T(8,128)}, f32[8,128,16,128]{3,2,1,0:T(8,128)}) custom-call(f32[8,128,16,128]{3,2,1,0:T(8,128)S(1)} %get-tuple-element.5.end, f32[8,128,16,128]{3,2,1,0:T(8,128)S(1)} %get-tuple-element.6.scan, f32[8,128,128]{2,1,0:T(8,128)S(1)} %get-tuple-element.7.base), custom_call_target="tpu_custom_call" | custom-call | tf_op jit(solution)/shard_map/pallas_call | solution.py:479

commit v5 on v4

--- a/solution.py
+++ b/solution.py
@@ -22,7 +22,7 @@
 
 
 def faces_first(level, rows):
-    return min(1 if level == 0 else 2 + 2 * level, rows)
+    return min(2 + 2 * level, rows)
 
 
 def tops_before(level, levels, rows, at):
@@ -34,18 +34,14 @@
 
 
 def last_plan(level, levels, rows):
-    plan, face, top = [], faces_first(level, rows), 0
+    plan, top = [], 0
     for at in range(rows):
-        while level > 0 and top < tops_before(level, levels, rows, at):
+        while top < tops_before(level, levels, rows, at):
             plan.append(("top", top))
             top += 1
         plan.append(("sum", at))
-        if at in (2, 4) and face < rows:
-            plan.append(("face", face))
-            face += 1
-    plan += [("face", at) for at in range(face, rows)]
-    if level > 0:
-        plan += [("top", at) for at in range(top, rows)]
+    plan += [("face", at) for at in range(faces_first(level, rows), rows)]
+    plan += [("top", at) for at in range(top, rows)]
     return plan
 
 
@@ -85,11 +81,10 @@
         return pltpu.make_async_copy(f_hbm.at[rows], field.at[0, rows, pl.ds(0, X)], in_sem.at[group])
 
     inner = pl.ds(1, Y - 2)
-    first_faces = face_in(pl.ds(0, 1), 0)
-    other_faces = face_in(pl.ds(1, Y - 1), 1)
+    faces_in = [face_in(pl.ds(0, 1), 0), face_in(pl.ds(Y - 1, 1), 1), face_in(inner, 2)]
     f_in = [field_in(pl.ds(0, 1), 0), field_in(pl.ds(Y - 1, 1), 1), field_in(inner, 2)]
     c_in = pltpu.make_async_copy(c_hbm, crowd, in_sem.at[3])
-    for copy in first_faces + other_faces + f_in:
+    for copy in faces_in[0] + faces_in[1] + faces_in[2] + f_in:
         copy.start()
     c_in.start()
 
@@ -159,10 +154,25 @@
             send(row.at[X - 1], lon.at[s, y, 0], lon_send.at[s], lon_recv.at[s, y], "lon", 1),
         ]
 
+    def start_lon(y, wrap):
+        low, high = lon_copies(0, y)
+        end = sizes["lon"] - 1
+
+        @pl.when((places["lon"] == 0) if wrap else (places["lon"] > 0))
+        def _():
+            low.start()
+
+        @pl.when((places["lon"] == end) if wrap else (places["lon"] < end))
+        def _():
+            high.start()
+
     def send_plane(t, y):
-        s = t % 2
         for copy in lon_copies(t, y):
             copy.start()
+        send_lat(t, y)
+
+    def send_lat(t, y):
+        s = t % 2
         if y == 0:
             send(field.at[s, 0, pl.ds(0, X)], lat.at[s, 1], lat_send.at[s], lat_recv.at[s], "lat", -1).start()
         if y == Y - 1:
@@ -186,24 +196,28 @@
         def _():
             down(0, y, lev_recv.at[0, y]).start()
 
-    for copy in first_faces:
-        copy.wait()
-    start_level(0, False)
-    for copy in other_faces:
-        copy.wait()
+    def face_wait(group):
+        for copy in faces_in[group]:
+            copy.wait()
+
     ahead = Y // 2
-    for y in order[1:ahead]:
-        start_level(y, False)
+    for at in range(2):
+        face_wait(at)
+        start_level(order[at], False)
 
     @pl.when((level > 0) & (level < levels - 1))
     def _():
-        for y in order[ahead:]:
+        meet_ends("lev")
+        face_wait(2)
+        for y in order[2:]:
             start_level(y, False)
-
-    meet_ends("lev")
 
     @pl.when((level == 0) | (level == levels - 1))
     def _():
+        face_wait(2)
+        for y in order[2:ahead]:
+            start_level(y, False)
+        meet_ends("lev")
         for y in order[:ahead]:
             start_level(y, True)
         for y in order[ahead:]:
@@ -212,9 +226,13 @@
 
     for copy in f_in:
         copy.wait()
+    for y in (0, Y - 1):
+        send_lat(0, y)
+    for y in order:
+        start_lon(y, False)
     meet_ends("lon")
     for y in order:
-        send_plane(0, y)
+        start_lon(y, True)
 
     @pl.when(level == 0)
     def _():
@@ -329,11 +347,10 @@
                     def _():
                         last_up(y).start()
 
-            if at < faces_first(0, Y):
+            if at < 2:
                 @pl.when(level == 0)
                 def _():
                     last_down(y).start()
-                    last_up(y).start()
 
             done = set(order[: at + 1])
             earlier = set(order[:at])
@@ -349,22 +366,14 @@
                 @pl.when(level == 0)
                 def _():
                     send_sum(row, False)
-                    plan = last_plan(0, levels, Y)
-                    here = plan.index(("sum", place_of))
-                    for kind, which in plan[here + 1 : here + 2]:
-                        if kind == "face" and place_of < Y - 1:
-                            last_down(order[which]).start()
-                            last_up(order[which]).start()
+                    if 2 <= place_of < Y - 2:
+                        last_down(row).start()
 
     @pl.when(level == 0)
     def _():
-        plan = last_plan(0, levels, Y)
-        left = [order[which] for kind, which in plan[plan.index(("sum", Y - 1)) + 1 :]]
-        for at, y in enumerate(left):
-            if at == 0:
-                last_down(y).start()
-            if at + 1 < len(left):
-                last_down(left[at + 1]).start()
+        for y in order[max(Y - 2, 2) :]:
+            last_down(y).start()
+        for y in order:
             last_up(y).start()
 
     for k in range(1, levels - 1):
@@ -459,7 +468,7 @@
             pltpu.VMEM((Y, X, L), f32),
             pltpu.VMEM((Y, X, L), f32),
             dma((4,)),
-            dma((2, 2)),
+            dma((3, 2)),
             dma((2,)),
             dma((2,)),
             dma((2,)),

time: 113 us -> 112 us (level)
    pallas_call x1, Pallas kernels: 106 us -> 105 us  [per_device(): pl.pallas_call(functools.partial(march, sizes), out_shape=(pltpu.VMEM((Y,...]
where the time goes in v5:
time: 112 us; the launch traced here: 111 us
  Pallas kernels  111 us (99%)
    pallas_call x1, Pallas kernels, per_device(): pl.pallas_call(functools.partial(march, sizes), out_shape=(pltpu.VMEM((Y,...  105 us
    pallas_call x1, Pallas kernels, per_device(): pl.pallas_call(functools.partial(finish, 1.0 / (Z * sizes['lev'])), out_s...  5.96 us

profile of v5, /device:TPU:24, one launch (start us, length us, event | category | flops | bytes accessed | tf_op | source)
XLA Modules:
  0.0 111.4 jit_solution(8187061063002317068)
XLA Ops:
  0.6 104.8 %shard_map.41 = (f32[8,128,16,128]{3,2,1,0:T(8,128)S(1)}, f32[8,128,16,128]{3,2,1,0:T(8,128)S(1)}, f32[8,128,128]{2,1,0:T(8,128)S(1)}) custom-call(f32[8,128,16,128]{3,2,1,0:T(8,128)} %f_hbm.1, f32[8,128,16,128]{3,2,1,0:T(8,128)} %c_hbm.1), custom_call_target="tpu_custom_call" | custom-call | tf_op jit(solution)/shard_map/pallas_call | solution.py:455
  105.4 6.0 %shard_map.42 = (f32[8,128,16,128]{3,2,1,0:T(8,128)}, f32[8,128,16,128]{3,2,1,0:T(8,128)}) custom-call(f32[8,128,16,128]{3,2,1,0:T(8,128)S(1)} %get-tuple-element.5.end, f32[8,128,16,128]{3,2,1,0:T(8,128)S(1)} %get-tuple-element.6.scan, f32[8,128,128]{2,1,0:T(8,128)S(1)} %get-tuple-element.7.base), custom_call_target="tpu_custom_call" | custom-call | tf_op jit(solution)/shard_map/pallas_call | solution.py:488

commit v6 on v5

--- a/solution.py
+++ b/solution.py
@@ -21,28 +21,39 @@
     return order
 
 
-def faces_first(level, rows):
-    return min(2 + 2 * level, rows)
-
-
-def tops_before(level, levels, rows, at):
-    if level == levels - 2:
-        return min(at + 3, rows)
-    if level == levels - 3:
-        return max(min(2 * (at - 3), rows - 2), 0)
-    return 0
+def holds(level):
+    return 0 if level == 0 else 1
 
 
 def last_plan(level, levels, rows):
-    plan, top = [], 0
-    for at in range(rows):
-        while top < tops_before(level, levels, rows, at):
-            plan.append(("top", top))
+    all_rows = list(range(rows))
+    steps = [[] for _ in all_rows]
+
+    def these(kind, places):
+        return [(kind, at) for at in places]
+
+    if level == levels - 1:
+        for at in all_rows:
+            steps[at].append(("top", at))
+        return steps, these("low", all_rows)
+    if level == 0:
+        steps[0].append(("low", 0))
+        end = []
+        for at in all_rows[1:]:
+            end += [("low", at), ("up", at - 1)]
+        return steps, end + [("up", rows - 1)]
+    near_top = level == levels - 2
+    early_ups = rows // 2 if level == 1 and not near_top else 3 * rows // 4
+    early_lows = rows // 2 if near_top else rows
+    for at in all_rows:
+        steps[at] += these("up", [at] if at < early_ups else []) + these("low", [at] if at < early_lows else [])
+    end, top = [], 0
+    for at in all_rows:
+        while near_top and top < min(at + 2, rows):
+            end.append(("top", top))
             top += 1
-        plan.append(("sum", at))
-    plan += [("face", at) for at in range(faces_first(level, rows), rows)]
-    plan += [("top", at) for at in range(top, rows)]
-    return plan
+        end.append(("sum", at))
+    return steps, end + these("top", all_rows[top:]) + these("up", all_rows[early_ups:]) + these("low", all_rows[early_lows:])
 
 
 def march(
@@ -56,6 +67,7 @@
     level = lax.axis_index("lev")
     levels = sizes["lev"]
     LAST = STEPS - 1
+    gives_way = lax.axis_index("lat") == sizes["lat"] - 1
     upper_part = jnp.where(level > 0, 0.1, 0.0).astype(jnp.float32)
 
     def beside(axis, shift):
@@ -71,21 +83,13 @@
     def arrived(ref, sem):
         pltpu.make_async_copy(ref, ref, sem).wait()
 
-    def face_in(rows, group):
-        return [
-            pltpu.make_async_copy(f_hbm.at[rows, :, 0], face.at[0, 0, rows], face_sem.at[group, 0]),
-            pltpu.make_async_copy(f_hbm.at[rows, :, Z - 1], face.at[0, 1, rows], face_sem.at[group, 1]),
-        ]
-
-    def field_in(rows, group):
-        return pltpu.make_async_copy(f_hbm.at[rows], field.at[0, rows, pl.ds(0, X)], in_sem.at[group])
-
-    inner = pl.ds(1, Y - 2)
-    faces_in = [face_in(pl.ds(0, 1), 0), face_in(pl.ds(Y - 1, 1), 1), face_in(inner, 2)]
-    f_in = [field_in(pl.ds(0, 1), 0), field_in(pl.ds(Y - 1, 1), 1), field_in(inner, 2)]
-    c_in = pltpu.make_async_copy(c_hbm, crowd, in_sem.at[3])
-    for copy in faces_in[0] + faces_in[1] + faces_in[2] + f_in:
-        copy.start()
+    groups = [pl.ds(0, 1), pl.ds(Y - 1, 1), pl.ds(1, Y - 2)]
+    f_in = pltpu.make_async_copy(f_hbm, field.at[0, :, pl.ds(0, X)], in_sem.at[0])
+    c_in = pltpu.make_async_copy(c_hbm, crowd, in_sem.at[1])
+    for group, rows in enumerate(groups):
+        pltpu.make_async_copy(f_hbm.at[rows, :, 0], face.at[0, 0, rows], face_sem.at[group]).start()
+        pltpu.make_async_copy(f_hbm.at[rows, :, Z - 1], face.at[0, 1, rows], face_sem.at[group]).start()
+    f_in.start()
     c_in.start()
 
     places = {axis: lax.axis_index(axis) for axis in ("lev", "lon")}
@@ -137,10 +141,10 @@
                 signal(ends_sem.at[at, 1], axis, -1)
 
     def down(t, y, sem):
-        return send(face.at[t, 0, y], lev.at[t % 2, y, 1], lev_send.at[t], sem, "lev", -1)
+        return send(face.at[t, 0, y], lev.at[t % 2, y, 1], lev_send, sem, "lev", -1)
 
     def up(t, y, sem):
-        return send(face.at[t, 1, y], lev.at[t % 2, y, 0], lev_send.at[t], sem, "lev", 1)
+        return send(face.at[t, 1, y], lev.at[t % 2, y, 0], lev_send, sem, "lev", 1)
 
     def send_level(t, y):
         up(t, y, lev_recv.at[t % 2, y]).start()
@@ -197,8 +201,7 @@
             down(0, y, lev_recv.at[0, y]).start()
 
     def face_wait(group):
-        for copy in faces_in[group]:
-            copy.wait()
+        arrived(face.at[0, :, groups[group]], face_sem.at[group])
 
     ahead = Y // 2
     for at in range(2):
@@ -224,8 +227,7 @@
             start_level(y, False)
             start_level(y, True)
 
-    for copy in f_in:
-        copy.wait()
+    f_in.wait()
     for y in (0, Y - 1):
         send_lat(0, y)
     for y in order:
@@ -315,12 +317,31 @@
         return up(LAST, y, lev_recv.at[LAST % 2, y])
 
     def send_top(y):
-        send(face.at[LAST, 1, y], top.at[y], lev_send.at[LAST], top_recv.at[y], "lev", -1).start()
+        send(face.at[LAST, 1, y], top.at[y], lev_send, top_recv.at[y], "lev", -1).start()
 
     def relay_top(y):
         copy = send(top.at[y], top.at[y], top_send, top_recv.at[y], "lev", -1)
         copy.wait_recv()
         copy.start()
+
+    plans = [last_plan(k, levels, Y) for k in range(levels)]
+
+    def act(k, kind, which):
+        y = order[which]
+        if kind == "sum":
+            send_sum(y, True)
+        elif kind == "up" and which >= Y - holds(k):
+            @pl.when(~gives_way)
+            def _():
+                last_up(y).start()
+        elif kind == "up":
+            last_up(y).start()
+        elif kind == "low":
+            last_down(y).start()
+        elif k == levels - 1:
+            send_top(y)
+        else:
+            relay_top(y)
 
     for t in range(LAST):
         if t >= 1:
@@ -333,24 +354,12 @@
             if t < LAST - 1:
                 continue
 
-            @pl.when(level == levels - 1)
-            def _():
-                send_top(y)
-
-            @pl.when(level > 0)
-            def _():
-                last_down(y).start()
-
-            for k in range(1, levels - 1):
-                if at < faces_first(k, Y):
+            for k in range(levels):
+                if plans[k][0][at]:
                     @pl.when(level == k)
                     def _():
-                        last_up(y).start()
-
-            if at < 2:
-                @pl.when(level == 0)
-                def _():
-                    last_down(y).start()
+                        for kind, which in plans[k][0][at]:
+                            act(k, kind, which)
 
             done = set(order[: at + 1])
             earlier = set(order[:at])
@@ -361,35 +370,19 @@
             ]
             for row in ready:
                 last_row(row)
-                place_of = order.index(row)
 
                 @pl.when(level == 0)
                 def _():
                     send_sum(row, False)
-                    if 2 <= place_of < Y - 2:
-                        last_down(row).start()
-
-    @pl.when(level == 0)
-    def _():
-        for y in order[max(Y - 2, 2) :]:
-            last_down(y).start()
-        for y in order:
-            last_up(y).start()
-
-    for k in range(1, levels - 1):
+
+    for k in range(levels):
         @pl.when(level == k)
         def _():
-            for kind, which in last_plan(k, levels, Y):
-                y = order[which]
-                if kind == "sum":
-                    send_sum(y, True)
-                elif kind == "face":
-                    last_up(y).start()
-                else:
-                    relay_top(y)
+            for kind, which in plans[k][1]:
+                act(k, kind, which)
 
     now = LAST % 2
-    for y in order:
+    for at, y in enumerate(order):
         @pl.when(level == levels - 1)
         def _():
             sum_copy(y).wait_recv()
@@ -399,13 +392,23 @@
         def _():
             arrived(top.at[y], top_recv.at[y])
             lev[now, y, 0] = top[y]
+
+        base[y] = (below[y] + upper_part * face[LAST, 0, y]) + 0.1 * top[y]
+
+        @pl.when(level == 0)
+        def _():
             last_down(y).wait_recv()
 
         @pl.when(level > 0)
         def _():
             arrived(lev.at[now, y], lev_recv.at[now, y])
 
-        base[y] = (below[y] + upper_part * face[LAST, 0, y]) + 0.1 * top[y]
+        if at == max(Y - 3, 0):
+            for k in range(levels - 1):
+                @pl.when((level == k) & gives_way)
+                def _():
+                    for held in order[Y - holds(k) :]:
+                        last_up(held).start()
 
         for start in range(0, X, PIECE):
             some = pl.ds(start, PIECE)
@@ -422,8 +425,7 @@
     def _():
         arrived(top, top_send)
 
-    for t in range(STEPS):
-        arrived(face.at[t], lev_send.at[t])
+    arrived(face, lev_send)
     for t in (LAST - 1, LAST):
         plane_sent(t)
 
@@ -467,13 +469,13 @@
             pltpu.VMEM((Y, X, L), f32),
             pltpu.VMEM((Y, X, L), f32),
             pltpu.VMEM((Y, X, L), f32),
-            dma((4,)),
-            dma((3, 2)),
+            dma((2,)),
+            dma((3,)),
             dma((2,)),
             dma((2,)),
             dma((2,)),
             dma((2, Y)),
-            dma((STEPS,)),
+            dma,
             dma((2, Y)),
             dma,
             dma((Y,)),

time: 112 us -> 112 us (level)
  no operation moved by 1% of the time
where the time goes in v6:
time: 112 us; the launch traced here: 111 us
  Pallas kernels  110 us (98%)
    pallas_call x1, Pallas kernels, per_device(): pl.pallas_call(functools.partial(march, sizes), out_shape=(pltpu.VMEM((Y,...  104 us
    pallas_call x1, Pallas kernels, per_device(): pl.pallas_call(functools.partial(finish, 1.0 / (Z * sizes['lev'])), out_s...  5.96 us

profile of v6, /device:TPU:24, one launch (start us, length us, event | category | flops | bytes accessed | tf_op | source)
XLA Modules:
  0.0 111.0 jit_solution(7563479078869169796)
XLA Ops:
  0.6 104.4 %shard_map.41 = (f32[8,128,16,128]{3,2,1,0:T(8,128)S(1)}, f32[8,128,16,128]{3,2,1,0:T(8,128)S(1)}, f32[8,128,128]{2,1,0:T(8,128)S(1)}) custom-call(f32[8,128,16,128]{3,2,1,0:T(8,128)} %f_hbm.1, f32[8,128,16,128]{3,2,1,0:T(8,128)} %c_hbm.1), custom_call_target="tpu_custom_call" | custom-call | tf_op jit(solution)/shard_map/pallas_call | solution.py:457
  105.0 6.0 %shard_map.42 = (f32[8,128,16,128]{3,2,1,0:T(8,128)}, f32[8,128,16,128]{3,2,1,0:T(8,128)}) custom-call(f32[8,128,16,128]{3,2,1,0:T(8,128)S(1)} %get-tuple-element.5.end, f32[8,128,16,128]{3,2,1,0:T(8,128)S(1)} %get-tuple-element.6.scan, f32[8,128,128]{2,1,0:T(8,128)S(1)} %get-tuple-element.7.base), custom_call_target="tpu_custom_call" | custom-call | tf_op jit(solution)/shard_map/pallas_call | solution.py:490

commit v7 on v6

--- a/solution.py
+++ b/solution.py
@@ -40,7 +40,7 @@
         steps[0].append(("low", 0))
         end = []
         for at in all_rows[1:]:
-            end += [("low", at), ("up", at - 1)]
+            end += [("up", at - 1), ("low", at)]
         return steps, end + [("up", rows - 1)]
     near_top = level == levels - 2
     early_ups = rows // 2 if level == 1 and not near_top else 3 * rows // 4
@@ -432,8 +432,11 @@
 
 def finish(scale, end, scan, base, pot_hbm, end_hbm, pot, out_sem):
     Y, X, Z, L = pot.shape
-    ends = pltpu.make_async_copy(end, end_hbm, out_sem.at[0])
-    ends.start()
+    part = X // 4
+    for y in range(Y):
+        for x in range(0, X, part):
+            some = pl.ds(x, part)
+            pltpu.make_async_copy(end.at[y, some], end_hbm.at[y, some], out_sem.at[0]).start()
     for y in range(Y):
         @pl.loop(0, X // BLOCK)
         def _(at):
@@ -442,8 +445,10 @@
                 x = start + i
                 pot[y, x] = (scan[y, x] + base[y, pl.ds(x, 1), :]) * scale
 
-        pltpu.make_async_copy(pot.at[y], pot_hbm.at[y], out_sem.at[1]).start()
-    ends.wait()
+        for x in range(0, X, part):
+            some = pl.ds(x, part)
+            pltpu.make_async_copy(pot.at[y, some], pot_hbm.at[y, some], out_sem.at[1]).start()
+    pltpu.make_async_copy(end, end_hbm, out_sem.at[0]).wait()
     pltpu.make_async_copy(pot, pot_hbm, out_sem.at[1]).wait()
 
 

time: 112 us -> 111 us (level)
  no operation moved by 1% of the time
where the time goes in v7:
time: 111 us
  Pallas kernels  110 us (99%)
    pallas_call x1, Pallas kernels, per_device(): pl.pallas_call(functools.partial(march, sizes), out_shape=(pltpu.VMEM((Y,...  105 us
    pallas_call x1, Pallas kernels, per_device(): pl.pallas_call(functools.partial(finish, 1.0 / (Z * sizes['lev'])), out_s...  5.78 us

profile of v7, /device:TPU:24, one launch (start us, length us, event | category | flops | bytes accessed | tf_op | source)
XLA Modules:
  0.0 111.0 jit_solution(3069266853220428975)
XLA Ops:
  0.6 104.6 %shard_map.41 = (f32[8,128,16,128]{3,2,1,0:T(8,128)S(1)}, f32[8,128,16,128]{3,2,1,0:T(8,128)S(1)}, f32[8,128,128]{2,1,0:T(8,128)S(1)}) custom-call(f32[8,128,16,128]{3,2,1,0:T(8,128)} %f_hbm.1, f32[8,128,16,128]{3,2,1,0:T(8,128)} %c_hbm.1), custom_call_target="tpu_custom_call" | custom-call | tf_op jit(solution)/shard_map/pallas_call | solution.py:462
  105.2 5.8 %shard_map.42 = (f32[8,128,16,128]{3,2,1,0:T(8,128)}, f32[8,128,16,128]{3,2,1,0:T(8,128)}) custom-call(f32[8,128,16,128]{3,2,1,0:T(8,128)S(1)} %get-tuple-element.5.end, f32[8,128,16,128]{3,2,1,0:T(8,128)S(1)} %get-tuple-element.6.scan, f32[8,128,128]{2,1,0:T(8,128)S(1)} %get-tuple-element.7.base), custom_call_target="tpu_custom_call" | custom-call | tf_op jit(solution)/shard_map/pallas_call | solution.py:495

commit v8 on v7

--- a/solution.py
+++ b/solution.py
@@ -53,7 +53,7 @@
             end.append(("top", top))
             top += 1
         end.append(("sum", at))
-    return steps, end + these("top", all_rows[top:]) + these("up", all_rows[early_ups:]) + these("low", all_rows[early_lows:])
+    return steps, end + these("up", all_rows[early_ups:]) + these("top", all_rows[top:]) + these("low", all_rows[early_lows:])
 
 
 def march(

time: 111 us -> 111 us (level)
  no operation moved by 1% of the time
where the time goes in v8:
time: 111 us
  Pallas kernels  110 us (99%)
    pallas_call x1, Pallas kernels, per_device(): pl.pallas_call(functools.partial(march, sizes), out_shape=(pltpu.VMEM((Y,...  105 us
    pallas_call x1, Pallas kernels, per_device(): pl.pallas_call(functools.partial(finish, 1.0 / (Z * sizes['lev'])), out_s...  5.78 us

profile of v8, /device:TPU:24, one launch (start us, length us, event | category | flops | bytes accessed | tf_op | source)
XLA Modules:
  0.0 111.0 jit_solution(16721508702170164015)
XLA Ops:
  0.6 104.6 %shard_map.41 = (f32[8,128,16,128]{3,2,1,0:T(8,128)S(1)}, f32[8,128,16,128]{3,2,1,0:T(8,128)S(1)}, f32[8,128,128]{2,1,0:T(8,128)S(1)}) custom-call(f32[8,128,16,128]{3,2,1,0:T(8,128)} %f_hbm.1, f32[8,128,16,128]{3,2,1,0:T(8,128)} %c_hbm.1), custom_call_target="tpu_custom_call" | custom-call | tf_op jit(solution)/shard_map/pallas_call | solution.py:462
  105.2 5.8 %shard_map.42 = (f32[8,128,16,128]{3,2,1,0:T(8,128)}, f32[8,128,16,128]{3,2,1,0:T(8,128)}) custom-call(f32[8,128,16,128]{3,2,1,0:T(8,128)S(1)} %get-tuple-element.5.end, f32[8,128,16,128]{3,2,1,0:T(8,128)S(1)} %get-tuple-element.6.scan, f32[8,128,128]{2,1,0:T(8,128)S(1)} %get-tuple-element.7.base), custom_call_target="tpu_custom_call" | custom-call | tf_op jit(solution)/shard_map/pallas_call | solution.py:495
